TPU v7x, 32 devices: a whole 2x2x4 slice. The times are simulated.
32 devices in a mesh: section: 2 (over core), expert: 16 (over z, y, x).
Axes of the slice: x: 2, y: 2, z: 4, core: 2. Of those that a mesh axis runs over, the one named last changes fastest.
Arguments:
- grad_out: bfloat16 [2, 2048, 4096], P('section', 'expert'), may hold values from -6 to 6
- saved_hidden: bfloat16 [2, 2048, 8, 1024], P('section', 'expert'), may hold values from -6 to 6
- routes: int32 [2, 2048, 8], P('section', 'expert'), may hold values from 0 to 15, all different within a row; in each aligned block of 128 rows (0 to 127, 128 to 255, ..., all dimensions but the last counted through in order) at most 96 rows name the same one
- scores: float32 [2, 2048, 8], P('section', 'expert'), may hold values from 0.02 to 0.98
- down_weight: bfloat16 [2, 16, 1024, 4096], P('section', 'expert'), may hold values from -0.1875 to 0.1875
- router: bfloat16 [2, 16, 4096], P('section'), may hold values from -0.59765625 to 0.59765625
Outputs:
- weight_grad: bfloat16 [2, 16, 1024, 4096], P('section', 'expert')
- handed: bfloat16 [2, 2048, 4096], P('section', 'expert')
Inputs may be any that keep to these rules, and one draw needn't show every extreme that they name: `routes`: each token names 8 different experts. Among the 128 tokens of one index of expert (aligned blocks), no expert is named more than 96 times, and in every draw some expert is named exactly 96 times in some block.
All inputs are finite; a program needn't handle non-finite values.
Results may differ from a plain program's by a relative error of at most 0.007.
Values may be sent and summed in bfloat16 or wider, within the bound.
A program may use at most 128 MiB of HBM per device.

v0:
```python
import jax
import jax.numpy as jnp
from jax import lax
from jax.sharding import PartitionSpec as P


def passed_along(array, axis, by):
    size = lax.axis_size(axis)
    return lax.ppermute(array, axis, [(i, (i + by) % size) for i in range(size)])


def slot_layout(route_ids, n_experts, capacity):
    flat_routes = route_ids.reshape(-1)
    entries = flat_routes.shape[0]
    onehot = (flat_routes[:, None] == jnp.arange(n_experts, dtype=jnp.int32)[None, :]).astype(
        jnp.int32
    )
    running = jnp.cumsum(onehot, axis=0)
    slot_index = jnp.sum(running * onehot, axis=1) - 1
    target = flat_routes * capacity + slot_index
    source = jnp.full((n_experts * capacity,), entries, jnp.int32)
    source = source.at[target].set(jnp.arange(entries, dtype=jnp.int32))
    return (target, source)


def expert_derivs(grad_in, hidden_in, expert_down):
    projected = lax.dot_general(
        grad_in, expert_down, (((1,), (1,)), ((), ())), preferred_element_type=jnp.float32
    )
    return jnp.sum(projected * hidden_in.astype(jnp.float32), axis=1)


def weight_pass(grad_in, hidden_in, weight_in):
    scaled = (weight_in.astype(jnp.float32)[:, None] * grad_in.astype(jnp.float32)).astype(
        jnp.bfloat16
    )
    weight_grads = lax.dot_general(
        hidden_in, scaled, (((0,), (0,)), ((), ())), preferred_element_type=jnp.float32
    )
    return weight_grads.astype(jnp.bfloat16)


def body(grad_out, saved_hidden, routes, scores, down_weight, router):
    grad_rows = grad_out[0]
    hidden_rows = saved_hidden[0]
    route_ids = routes[0]
    score_rows = scores[0]
    expert_down = down_weight[0, 0]
    router_rows = router[0]
    n_tokens, n_routes, hidden_width = hidden_rows.shape
    model_width = grad_rows.shape[1]
    n_experts = router_rows.shape[0]
    capacity = 3 * n_tokens * n_routes // (2 * n_experts)
    entries = n_tokens * n_routes
    target, source = slot_layout(route_ids, n_experts, capacity)
    filled = source < entries
    safe_index = jnp.minimum(source, entries - 1)
    score_total = jnp.sum(score_rows, axis=1, keepdims=True)
    weights = score_rows / score_total
    weights_low = weights.astype(jnp.bfloat16).reshape(-1)
    grad_slots = jnp.where(
        filled[:, None], grad_rows[safe_index // n_routes], jnp.zeros((), jnp.bfloat16)
    )
    grad_slots = grad_slots.reshape(n_experts, capacity, model_width)
    hidden_slots = jnp.where(
        filled[:, None],
        hidden_rows.reshape(entries, hidden_width)[safe_index],
        jnp.zeros((), jnp.bfloat16),
    )
    hidden_slots = hidden_slots.reshape(n_experts, capacity, hidden_width)
    weight_slots = jnp.where(filled, weights_low[safe_index], jnp.zeros((), jnp.bfloat16)).reshape(
        n_experts, capacity
    )
    grad_piece = lax.all_to_all(grad_slots, "expert", split_axis=0, concat_axis=0, tiled=True)
    hidden_piece = lax.all_to_all(hidden_slots, "expert", split_axis=0, concat_axis=0, tiled=True)
    weight_piece = lax.all_to_all(weight_slots, "expert", split_axis=0, concat_axis=0, tiled=True)
    n_source = grad_piece.shape[0]
    slot_count = grad_piece.shape[1]
    derivs = expert_derivs(
        grad_piece.reshape(-1, model_width), hidden_piece.reshape(-1, hidden_width), expert_down
    )
    sent_back = lax.all_to_all(
        derivs.reshape(n_source, slot_count), "expert", split_axis=0, concat_axis=0, tiled=True
    )
    weight_out = weight_pass(
        grad_piece.reshape(-1, model_width),
        hidden_piece.reshape(-1, hidden_width),
        weight_piece.reshape(-1),
    )
    derivs_home = sent_back.reshape(-1)[target].reshape(n_tokens, n_routes)
    center = jnp.sum(weights * derivs_home, axis=1, keepdims=True)
    logit_grad = score_rows * (1.0 - score_rows) / score_total * (derivs_home - center)
    expert_ids = jnp.arange(n_experts, dtype=jnp.int32)
    dense_grad = jnp.sum(
        jnp.where(route_ids[:, :, None] == expert_ids[None, None, :], logit_grad[:, :, None], 0.0),
        axis=1,
    )
    input_grad = grad_rows.astype(jnp.float32) + jnp.dot(
        dense_grad, router_rows.astype(jnp.float32), precision=lax.Precision.HIGHEST
    )
    handed = passed_along(input_grad.astype(jnp.bfloat16), "section", -1)
    return (weight_out[None, None], handed[None])


def solution(mesh):
    return jax.shard_map(
        body,
        mesh=mesh,
        in_specs=(
            P("section", "expert", None),
            P("section", "expert", None, None),
            P("section", "expert", None),
            P("section", "expert", None),
            P("section", "expert", None, None),
            P("section", None, None),
        ),
        out_specs=(P("section", "expert", None, None), P("section", "expert", None)),
        check_vma=False,
    )
```

profile of v0, /device:TPU:0, one launch (start us, length us, event | category | flops | bytes accessed | tf_op | source)
XLA Modules:
  0.0 471.2 jit_solution(10010152508864146253)
XLA Ops:
  0.6 0.8 broadcast_multiply_fusion
  1.5 0.8 copy.52
  2.5 0.1 copy.51
  2.6 0.1 mul.50
  2.7 4.5 reduce-window.6
  7.3 0.1 copy.54
  7.7 4.3 scatter_custom_fusion
  12.0 0.8 copy.56
  12.9 0.7 reduce_sum.46
  13.8 5.8 %gather_fusion = bf16[1536,1024]{1,0:T(8,128)(2,1)} fusion(bf16[1024,1024]{1,0:T(8,128)(2,1)S(1)} %bitcast.52, s32[2048]{0:T(1024)S(1)} %get-tuple-element.7), kind=kCustom, calls=%fused_computation | custom fusion | bytes 6297600 | tf_op jit(solution)/shard_map/gather | solution.py:67
  19.6 9.5 %gather_fusion.1 = bf16[1536]{0:T(1024)(128)(2,1)S(1)} fusion(bf16[1024]{0:T(1024)(128)(2,1)S(1)} %divide_convert_fusion, s32[2048]{0:T(1024)S(1)} %get-tuple-element.7), kind=kCustom, calls=%fused_computation.1 | custom fusion | bytes 12288 | tf_op jit(solution)/shard_map/gather | solution.py:71
  29.2 3.3 broadcast_select_fusion.1
  32.4 8.4 %all-to-all-start = ((bf16[16,96,1024]{2,1,0:T(8,128)(2,1)}), bf16[16,96,1024]{2,1,0:T(8,128)(2,1)}, u32[]{:S(2)}, u32[]{:S(2)}) async-start(bf16[16,96,1024]{2,1,0:T(8,128)(2,1)} %broadcast_select_fusion.1), calls=%async_computation | async-start | bytes 6291456 | tf_op jit(solution)/shard_map/all_to_all | solution.py:75
  40.8 9.5 %gather_fusion.2 = bf16[1536,4096]{1,0:T(8,128)(2,1)} fusion(bf16[128,4096]{1,0:T(8,128)(2,1)S(1)} %bitcast.53, s32[2048]{0:T(1024)S(1)} %get-tuple-element.6), kind=kCustom, calls=%fused_computation.2 | custom fusion | bytes 25171968 | tf_op jit(solution)/shard_map/gather | solution.py:62
  50.4 10.6 %broadcast_select_fusion = bf16[16,96,4096]{2,1,0:T(8,128)(2,1)} fusion(bf16[16,96,4096]{2,1,0:T(8,128)(2,1)} %bitcast.54, pred[16,96]{1,0:T(8,128)(4,1)S(1)} %broadcast_in_dim.65), kind=kLoop, calls=%fused_computation.9 | loop fusion | flops 6291456 | bytes 25167360 | tf_op jit(solution)/shard_map/jit(_where)/select_n | solution.py:61
  61.0 40.8 %all-to-all-done = bf16[16,96,1024]{2,1,0:T(8,128)(2,1)} async-done(((bf16[16,96,1024]{2,1,0:T(8,128)(2,1)}), bf16[16,96,1024]{2,1,0:T(8,128)(2,1)}, u32[]{:S(2)}, u32[]{:S(2)}) %all-to-all-start) | async-done | bytes 3145760 | tf_op jit(solution)/shard_map/all_to_all | solution.py:75
  101.7 15.2 %all-to-all-start.2 = ((bf16[16,96,4096]{2,1,0:T(8,128)(2,1)}), bf16[16,96,4096]{2,1,0:T(8,128)(2,1)}, u32[]{:S(2)}, u32[]{:S(2)}) async-start(bf16[16,96,4096]{2,1,0:T(8,128)(2,1)} %broadcast_select_fusion), calls=%async_computation.2 | async-start | bytes 25165824 | tf_op jit(solution)/shard_map/all_to_all | solution.py:74
  116.9 0.7 all_to_all.24
  117.6 5.3 %bitcast_convert_fusion.1 = f32[1536,1024]{1,0:T(8,128)} fusion(bf16[16,96,1024]{2,1,0:T(8,128)(2,1)} %all-to-all-done), kind=kLoop, calls=%fused_computation.16 | loop fusion | flops 1572864 | bytes 9437184 | tf_op jit(solution)/shard_map/convert_element_type | solution.py:30
  122.9 6.7 %copy.59 = f32[1536,1024]{0,1:T(8,128)} copy(f32[1536,1024]{1,0:T(8,128)} %bitcast_convert_fusion.1) | data formatting | bytes 12582912 | tf_op jit(solution)/shard_map/convert_element_type | solution.py:30
  129.6 222.2 %all-to-all-done.2 = bf16[16,96,4096]{2,1,0:T(8,128)(2,1)} async-done(((bf16[16,96,4096]{2,1,0:T(8,128)(2,1)}), bf16[16,96,4096]{2,1,0:T(8,128)(2,1)}, u32[]{:S(2)}, u32[]{:S(2)}) %all-to-all-start.2) | async-done | bytes 12582944 | tf_op jit(solution)/shard_map/all_to_all | solution.py:74
  351.8 55.5 %all-to-all-start.1 = ((bf16[16,1,96]{2,1,0:T(2,128)(2,1)}), bf16[16,1,96]{2,1,0:T(2,128)(2,1)S(1)}, u32[]{:S(2)}, u32[]{:S(2)}) async-start(bf16[16,1,96]{2,1,0:T(2,128)(2,1)} %all_to_all.24), calls=%async_computation.1 | async-start | bytes 16384 | tf_op jit(solution)/shard_map/all_to_all | solution.py:76
  407.4 18.9 %multiply_reduce_fusion = f32[1536]{0:T(1024)S(1)} fusion(f32[1536,1024]{0,1:T(8,128)} %copy.59, bf16[1536,4096]{1,0:T(8,128)(2,1)} %bitcast.13, bf16[1,1,1024,4096]{3,2,1,0:T(8,128)(2,1)} %param.10), kind=kOutput, calls=%fused_computation.13 | convolution fusion | flops 12888045568 | bytes 27269120 | tf_op jit(solution)/shard_map/dot_general | solution.py:27
  426.3 0.7 all_to_all.22
  427.0 6.9 %all-to-all-start.3 = ((f32[16,1,96]{2,1,0:T(1,128)}), f32[16,1,96]{2,1,0:T(1,128)S(1)}, u32[]{:S(2)}, u32[]{:S(2)}) async-start(f32[16,1,96]{2,1,0:T(1,128)} %all_to_all.22), calls=%async_computation.3 | async-start | bytes 16384 | tf_op jit(solution)/shard_map/all_to_all | solution.py:82
  434.0 7.2 %all-to-all-done.3 = f32[16,1,96]{2,1,0:T(1,128)S(1)} async-done(((f32[16,1,96]{2,1,0:T(1,128)}), f32[16,1,96]{2,1,0:T(1,128)S(1)}, u32[]{:S(2)}, u32[]{:S(2)}) %all-to-all-start.3) | async-done | bytes 6176 | tf_op jit(solution)/shard_map/all_to_all | solution.py:82
  441.2 0.5 broadcast.143
  441.7 0.7 reduce.4
  442.4 6.1 %gather_fusion.3 = f32[1024]{0:T(1024)S(1)} fusion(f32[1536]{0:T(1024)S(1)} %reshape.157, s32[1024]{0:T(1024)S(1)} %broadcast_clamp_fusion), kind=kCustom, calls=%fused_computation.3 | custom fusion | bytes 12288 | tf_op jit(solution)/shard_map/gather | solution.py:90
  448.8 1.1 fusion.7
  450.0 20.2 %fusion.2 = bf16[1,1,1024,4096]{3,2,1,0:T(8,128)(2,1)} fusion(bf16[16,96,1024]{2,1,0:T(8,128)(2,1)} %all-to-all-done, bf16[16,96,4096]{2,1,0:T(8,128)(2,1)} %all-to-all-done.2, f32[16,96]{1,0:T(8,128)S(1)} %bitcast.63), kind=kOutput, calls=%fused_computation.10 | convolution fusion | flops 12907970560 | bytes 24123392 | tf_op jit(solution)/shard_map/dot_general | solution.py:37
  470.2 1.0 copy.65
  (43 shorter events, 1.3 us)
Async XLA Ops:
  0.6 13.2 %copy-start = (bf16[1,128,8,1024]{3,2,1,0:T(8,128)(2,1)S(1)}, bf16[1,128,8,1024]{3,2,1,0:T(8,128)(2,1)}, u32[]{:S(2)}) copy-start(bf16[1,128,8,1024]{3,2,1,0:T(8,128)(2,1)} %param.7) | copy-start | bytes 6291460
  19.6 21.2 %copy-start.2 = (bf16[1,128,4096]{2,1,0:T(8,128)(2,1)S(1)}, bf16[1,128,4096]{2,1,0:T(8,128)(2,1)}, u32[]{:S(2)}) copy-start(bf16[1,128,4096]{2,1,0:T(8,128)(2,1)} %param.6) | copy-start | bytes 3145732
  32.4 69.3 %all-to-all-start = ((bf16[16,96,1024]{2,1,0:T(8,128)(2,1)}), bf16[16,96,1024]{2,1,0:T(8,128)(2,1)}, u32[]{:S(2)}, u32[]{:S(2)}) async-start(bf16[16,96,1024]{2,1,0:T(8,128)(2,1)} %broadcast_select_fusion.1), calls=%async_computation | async-start | bytes 6291456 | tf_op jit(solution)/shard_map/all_to_all | solution.py:75
  101.7 250.0 %all-to-all-start.2 = ((bf16[16,96,4096]{2,1,0:T(8,128)(2,1)}), bf16[16,96,4096]{2,1,0:T(8,128)(2,1)}, u32[]{:S(2)}, u32[]{:S(2)}) async-start(bf16[16,96,4096]{2,1,0:T(8,128)(2,1)} %broadcast_select_fusion), calls=%async_computation.2 | async-start | bytes 25165824 | tf_op jit(solution)/shard_map/all_to_all | solution.py:74
  351.8 75.2 %all-to-all-start.1 = ((bf16[16,1,96]{2,1,0:T(2,128)(2,1)}), bf16[16,1,96]{2,1,0:T(2,128)(2,1)S(1)}, u32[]{:S(2)}, u32[]{:S(2)}) async-start(bf16[16,1,96]{2,1,0:T(2,128)(2,1)} %all_to_all.24), calls=%async_computation.1 | async-start | bytes 16384 | tf_op jit(solution)/shard_map/all_to_all | solution.py:76
  407.3 41.4 %copy-start.4 = (f32[1,128,8]{1,2,0:T(8,128)S(1)}, f32[1,128,8]{1,2,0:T(8,128)}, u32[]{:S(2)}) copy-start(f32[1,128,8]{1,2,0:T(8,128)} %param.9) | copy-start | bytes 12292
  407.3 41.4 %copy-start.5 = (s32[1,128,8]{1,2,0:T(8,128)S(1)}, s32[1,128,8]{1,2,0:T(8,128)}, u32[]{:S(2)}) copy-start(s32[1,128,8]{1,2,0:T(8,128)} %param.8) | copy-start | bytes 12292
  407.4 41.4 %copy-start.3 = (bf16[1,16,4096]{2,1,0:T(8,128)(2,1)S(1)}, bf16[1,16,4096]{2,1,0:T(8,128)(2,1)}, u32[]{:S(2)}) copy-start(bf16[1,16,4096]{2,1,0:T(8,128)(2,1)} %param.11) | copy-start | bytes 393220
  427.0 14.2 %all-to-all-start.3 = ((f32[16,1,96]{2,1,0:T(1,128)}), f32[16,1,96]{2,1,0:T(1,128)S(1)}, u32[]{:S(2)}, u32[]{:S(2)}) async-start(f32[16,1,96]{2,1,0:T(1,128)} %all_to_all.22), calls=%async_computation.3 | async-start | bytes 16384 | tf_op jit(solution)/shard_map/all_to_all | solution.py:82
  449.9 20.3 %collective-permute-start = (bf16[128,4096]{1,0:T(8,128)(2,1)S(1)}, bf16[128,4096]{1,0:T(8,128)(2,1)S(1)}, u32[]{:S(2)}, u32[]{:S(2)}) collective-permute-start(bf16[128,4096]{1,0:T(8,128)(2,1)S(1)} %fusion.7), channel_id=1, source_target_pairs={{0,16},{16,0},{1,17},{17,1},{2,18},{18,2},{3,19},{19,3},{4,20},{20... | collective-permute-start | bytes 3145736 | tf_op jit(solution)/shard_map/ppermute | solution.py:9
  450.0 21.2 %copy-start.1 = (bf16[1,128,8,1024]{3,2,1,0:T(8,128)(2,1)S(1)}, bf16[1,128,8,1024]{3,2,1,0:T(8,128)(2,1)}, u32[]{:S(2)}) copy-start(bf16[1,128,8,1024]{3,2,1,0:T(8,128)(2,1)} %param.7) | copy-start | bytes 6291460
where the time goes:
time: 472 us; the launch traced here: 471 us
  waiting for transfers between devices  270 us (57%)
  starting transfers between devices  86.1 us (18%)
  local copies, waits for them, and re-layouts  47.6 us (10%)
  matrix products  40.3 us (9%)
  other arithmetic  26.2 us (6%)
    all_to_all x1, waiting for transfers between devices, body(): lax.all_to_all(grad_slots, 'expert', split_axis=0, concat_axis=0, tiled=T...  222 us
    all_to_all x1, starting transfers between devices, body(): lax.all_to_all(weight_slots, 'expert', split_axis=0, concat_axis=0, tiled...  55.5 us
    all_to_all x1, waiting for transfers between devices, body(): lax.all_to_all(hidden_slots, 'expert', split_axis=0, concat_axis=0, tiled...  40.8 us
    dot_general x1, matrix products, weight_pass(): lax.dot_general(hidden_in, scaled, (((0,), (0,)), ((), ())), preferred_el...  20.2 us
    dot_general x1, matrix products, expert_derivs(): lax.dot_general(grad_in, expert_down, (((1,), (1,)), ((), ())), preferred...  18.9 us
    all_to_all x1, starting transfers between devices, body(): lax.all_to_all(grad_slots, 'expert', split_axis=0, concat_axis=0, tiled=T...  15.2 us
    select_n x1, other arithmetic, body(): jnp.where(filled[:, None], grad_rows[safe_index // n_routes], jnp.zeros((...  10.6 us
    gather x1, local copies, waits for them, and re-layouts, body(): grad_rows[safe_index // n_routes]  9.54 us
  transfers between devices with their start and end apart: 5, of which 3 were waited for; matrix products, arithmetic and copies ran while one was open for 15% of the time, Pallas kernels for 0%

commit v1 on v0

v1 whole, which is shorter than its diff:
```python
import functools

import jax
import jax.numpy as jnp
from jax import lax
from jax.experimental import pallas as pl
from jax.experimental.pallas import tpu as pltpu
from jax.sharding import PartitionSpec as P

MESH = pl.DeviceIdType.MESH


def torus_dims(n):
    dims = [1, 1, 1]
    at = 0
    while n > 1:
        factor = next(f for f in range(2, n + 1) if n % f == 0)
        dims[at % 3] *= factor
        n //= factor
        at += 1
    return tuple(dims)


def tree_edges(dims, order, flip):
    reached = [(0, 0, 0)]
    edges = []
    for axis in order:
        size = dims[axis]
        fresh = []
        for count, start in enumerate(reached):
            extra = (count + flip) % 2 if size % 2 == 0 else 0
            plus = (size - 1) // 2 + (1 - extra if size > 2 and size % 2 == 0 else 0)
            if size == 2:
                plus = 1
            minus = size - 1 - plus
            for step, hops in ((1, plus), (-1, minus)):
                place = start
                for _ in range(hops):
                    after = list(place)
                    after[axis] = (after[axis] + step) % size
                    after = tuple(after)
                    edges.append((place, axis, step, after))
                    fresh.append(after)
                    place = after
        reached = reached + fresh
    return edges


def plan(dims, orders):
    waiting = []
    for chunk, (order, flip) in enumerate(orders):
        edges = tree_edges(dims, order, flip)
        below = {}
        for parent, axis, step, child in reversed(edges):
            below[parent] = max(below.get(parent, 0), below.get(child, 0) + 1)
        for parent, axis, step, child in edges:
            waiting.append((chunk, parent, axis, step, child, below.get(child, 0)))
    arrival = {(chunk, (0, 0, 0)): 0 for chunk in range(len(orders))}
    free = {}
    issued = []
    while waiting:
        best = None
        for item in waiting:
            chunk, parent, axis, step, child, depth = item
            if (chunk, parent) not in arrival:
                continue
            begin = max(arrival[(chunk, parent)], free.get((axis, step), 0))
            key = (begin, -depth, chunk)
            if best is None or key < best[0]:
                best = (key, item)
        (begin, _, _), item = best
        waiting.remove(item)
        chunk, parent, axis, step, child, depth = item
        free[(axis, step)] = begin + 1
        arrival[(chunk, child)] = begin + 1.5
        issued.append((begin, item[:5]))
    issued.sort(key=lambda pair: pair[0])
    return [item for _, item in issued]


def flat(offset, dims):
    return (offset[0] * dims[1] + offset[1]) * dims[2] + offset[2]


def exchange_kernel(dims, sends, grad_ref, dense_ref, all_ref, got_ref, own, own_dense, g_send, g_recv, h_send, h_recv, local):
    n = dims[0] * dims[1] * dims[2]
    me = lax.axis_index("expert")
    here = (me // (dims[1] * dims[2]), (me // dims[2]) % dims[1], me % dims[2])

    def at(offset, sign):
        c = [(here[i] + sign * offset[i] + dims[i]) % dims[i] for i in range(3)]
        return (c[0] * dims[1] + c[1]) * dims[2] + c[2]

    load = pltpu.make_async_copy(grad_ref, own, local.at[0])
    load.start()
    load_dense = pltpu.make_async_copy(dense_ref.at[me], own_dense, local.at[1])
    load_dense.start()
    barrier = pltpu.get_barrier_semaphore()
    for i in range(1, n):
        pl.semaphore_signal(barrier, inc=1, device_id={"expert": (me + i) % n}, device_id_type=MESH)
    pl.semaphore_wait(barrier, n - 1)
    load.wait()

    offsets = [(a, b, c) for a in range(dims[0]) for b in range(dims[1]) for c in range(dims[2])]
    offsets = [o for o in offsets if o != (0, 0, 0)]

    def dense_copy(offset):
        k = flat(offset, dims)
        return pltpu.make_async_remote_copy(
            src_ref=dense_ref.at[at(offset, 1)],
            dst_ref=got_ref.at[me],
            send_sem=h_send.at[k],
            recv_sem=h_recv.at[k],
            device_id={"expert": at(offset, 1)},
            device_id_type=MESH,
        )

    def grad_copy(item):
        chunk, parent, axis, step, child = item
        source = at(parent, -1)
        move = [0, 0, 0]
        move[axis] = step
        k = flat(child, dims)
        return pltpu.make_async_remote_copy(
            src_ref=own.at[chunk] if parent == (0, 0, 0) else all_ref.at[source, chunk],
            dst_ref=all_ref.at[source, chunk],
            send_sem=g_send.at[k, chunk],
            recv_sem=g_recv.at[k, chunk],
            device_id={"expert": at(move, 1)},
            device_id_type=MESH,
        )

    def arrived(chunk, offset):
        k = flat(offset, dims)
        source = at(offset, -1)
        pltpu.make_async_copy(all_ref.at[source, chunk], all_ref.at[source, chunk], g_recv.at[k, chunk]).wait()

    seen = set()
    pending = list(offsets)
    copies = []
    dense_copies = []
    stores = []
    own_sends = sum(1 for item in sends if item[1] == (0, 0, 0))
    every = max(1, (len(sends) * 2 // 3 - own_sends) // max(1, len(pending)))
    for count, item in enumerate(sends):
        chunk, parent = item[0], item[1]
        if parent != (0, 0, 0) and (chunk, parent) not in seen:
            arrived(chunk, parent)
            seen.add((chunk, parent))
        copy = grad_copy(item)
        copy.start()
        copies.append(copy)
        if count >= own_sends and (count - own_sends) % every == 0 and pending:
            extra = dense_copy(pending.pop(0))
            extra.start()
            dense_copies.append(extra)
        if count == own_sends:
            store = pltpu.make_async_copy(own, all_ref.at[me], local.at[2])
            store.start()
            load_dense.wait()
            store_dense = pltpu.make_async_copy(own_dense, got_ref.at[me], local.at[3])
            store_dense.start()
            stores = [store, store_dense]
    for offset in pending:
        extra = dense_copy(offset)
        extra.start()
        dense_copies.append(extra)
    for offset in offsets:
        for chunk in range(own.shape[0]):
            if (chunk, offset) not in seen:
                arrived(chunk, offset)
    for copy in dense_copies:
        copy.wait_recv()
    for copy in dense_copies:
        copy.wait_send()
    for copy in copies:
        copy.wait_send()
    for store in stores:
        store.wait()


def exchange(grad_rows, dense):
    n, n_tokens, hidden_width = dense.shape
    width = grad_rows.shape[1]
    dims = torus_dims(n)
    orders = [((2, 1, 0), 0), ((1, 2, 0), 1), ((0, 2, 1), 0), ((0, 1, 2), 1)]
    chunks = len(orders)
    rows = n_tokens // chunks
    grad_chunks = grad_rows.reshape(chunks, rows, width)
    got, dense_got = pl.pallas_call(
        functools.partial(exchange_kernel, dims, plan(dims, orders)),
        out_shape=(
            jax.ShapeDtypeStruct((n, chunks, rows, width), grad_rows.dtype),
            jax.ShapeDtypeStruct(dense.shape, dense.dtype),
        ),
        in_specs=[pl.BlockSpec(memory_space=pl.ANY)] * 2,
        out_specs=(pl.BlockSpec(memory_space=pl.ANY), pl.BlockSpec(memory_space=pl.ANY)),
        scratch_shapes=[
            pltpu.VMEM((chunks, rows, width), grad_rows.dtype),
            pltpu.VMEM((n_tokens, hidden_width), dense.dtype),
            pltpu.SemaphoreType.DMA((n, chunks)),
            pltpu.SemaphoreType.DMA((n, chunks)),
            pltpu.SemaphoreType.DMA((n,)),
            pltpu.SemaphoreType.DMA((n,)),
            pltpu.SemaphoreType.DMA((4,)),
        ],
        compiler_params=pltpu.CompilerParams(collective_id=0, has_side_effects=True),
        name="exchange",
    )(grad_chunks, dense)
    return got.reshape(n * n_tokens, width), dense_got.reshape(n * n_tokens, hidden_width)


def spread_kernel(n_experts, group, top, hidden_ref, weight_ref, route_ref, out_ref):
    rows, cols = n_experts * group, group * top
    row = lax.broadcasted_iota(jnp.int32, (rows, cols), 0)
    col = lax.broadcasted_iota(jnp.int32, (rows, cols), 1)
    named = (row % group == col // top) & (row // group == route_ref[0])
    mix = jnp.where(named, weight_ref[0], 0.0).astype(jnp.bfloat16)
    for e in range(n_experts):
        part = jnp.dot(
            mix[e * group : (e + 1) * group], hidden_ref[...], preferred_element_type=jnp.float32
        )
        out_ref[e] = part.astype(jnp.bfloat16)


def spread(hidden_rows, weights_low, route_ids, n_experts):
    n_tokens, top, width = hidden_rows.shape
    group = 16
    steps = n_tokens // group
    cols = group * top
    return pl.pallas_call(
        functools.partial(spread_kernel, n_experts, group, top),
        grid=(steps,),
        out_shape=jax.ShapeDtypeStruct((n_experts, n_tokens, width), jnp.bfloat16),
        in_specs=[
            pl.BlockSpec((cols, width), lambda i: (i, 0)),
            pl.BlockSpec((1, 1, cols), lambda i: (i, 0, 0)),
            pl.BlockSpec((1, 1, cols), lambda i: (i, 0, 0)),
        ],
        out_specs=pl.BlockSpec((n_experts, group, width), lambda i: (0, i, 0)),
        name="spread",
    )(
        hidden_rows.reshape(n_tokens * top, width),
        weights_low.astype(jnp.float32).reshape(steps, 1, cols),
        route_ids.reshape(steps, 1, cols),
    )


def deriv_kernel(grad_ref, hidden_ref, down_ref, out_ref):
    projected = lax.dot_general(
        grad_ref[...], down_ref[...], (((1,), (1,)), ((), ())), preferred_element_type=jnp.float32
    )
    out_ref[...] = jnp.sum(projected * hidden_ref[...].astype(jnp.float32), axis=1, keepdims=True)


def derivs_of(grads, hidden, down):
    rows, width = grads.shape
    hidden_width = hidden.shape[1]
    tile = 512
    return pl.pallas_call(
        deriv_kernel,
        grid=(rows // tile,),
        out_shape=jax.ShapeDtypeStruct((rows, 1), jnp.float32),
        in_specs=[
            pl.BlockSpec((tile, width), lambda i: (i, 0)),
            pl.BlockSpec((tile, hidden_width), lambda i: (i, 0)),
            pl.BlockSpec((hidden_width, width), lambda i: (0, 0)),
        ],
        out_specs=pl.BlockSpec((tile, 1), lambda i: (i, 0)),
        compiler_params=pltpu.CompilerParams(vmem_limit_bytes=50 * 1024 * 1024),
        cost_estimate=pl.CostEstimate(
            flops=2 * rows * width * hidden_width, bytes_accessed=2 * rows * width, transcendentals=0
        ),
        name="derivs",
    )(grads, hidden, down)


def passed_along(array, axis, by):
    size = lax.axis_size(axis)
    return lax.ppermute(array, axis, [(i, (i + by) % size) for i in range(size)])


def body(grad_out, saved_hidden, routes, scores, down_weight, router):
    grad_rows = grad_out[0]
    hidden_rows = saved_hidden[0]
    route_ids = routes[0]
    score_rows = scores[0]
    n_tokens = grad_rows.shape[0]
    n_experts = router.shape[1]
    score_total = jnp.sum(score_rows, axis=1, keepdims=True)
    weights = score_rows / score_total
    weights_low = weights.astype(jnp.bfloat16)

    next_grad = passed_along(grad_rows, "section", -1)
    next_router = passed_along(router[0], "section", -1)
    dense = spread(hidden_rows, weights_low, route_ids, n_experts)
    grads, hidden = exchange(grad_rows, dense)
    derivs = derivs_of(grads, hidden, down_weight[0, 0])
    home = lax.all_to_all(
        derivs.reshape(n_experts, n_tokens), "expert", split_axis=0, concat_axis=0, tiled=True
    )
    weight_out = lax.dot_general(
        hidden, grads, (((0,), (0,)), ((), ())), preferred_element_type=jnp.float32
    ).astype(jnp.bfloat16)

    named = route_ids.T[None] == jnp.arange(n_experts, dtype=jnp.int32)[:, None, None]
    low = weights_low.astype(jnp.float32)
    score_dense = jnp.sum(jnp.where(named, score_rows.T[None], 0.0), axis=1)
    fix_dense = jnp.sum(jnp.where(named, (weights / low).T[None], 0.0), axis=1)
    weighted = home * fix_dense
    center = jnp.sum(weighted, axis=0, keepdims=True)
    total_row = score_total.T
    logit_dense = (1.0 - score_dense) * (weighted - score_dense / total_row * center)
    next_logit = passed_along(logit_dense, "section", -1)
    handed = next_grad.astype(jnp.float32) + lax.dot_general(
        next_logit,
        next_router.astype(jnp.float32),
        (((0,), (0,)), ((), ())),
        precision=lax.Precision.HIGHEST,
    )
    return (weight_out[None, None], handed.astype(jnp.bfloat16)[None])


def solution(mesh):
    return jax.shard_map(
        body,
        mesh=mesh,
        in_specs=(
            P("section", "expert", None),
            P("section", "expert", None, None),
            P("section", "expert", None),
            P("section", "expert", None),
            P("section", "expert", None, None),
            P("section", None, None),
        ),
        out_specs=(P("section", "expert", None, None), P("section", "expert", None)),
        check_vma=False,
    )
```

time: 472 us -> 342 us (0.72)
  Pallas kernels: 0 us -> 278 us
  waiting for transfers between devices: 270 us -> 6.57 us
  starting transfers between devices: 86.1 us -> 26.2 us
  local copies, waits for them, and re-layouts: 47.6 us -> 2.63 us
  other arithmetic: 26.2 us -> 2.33 us
  matrix products: 40.3 us -> 25.3 us
    pallas_call x0 -> x3, Pallas kernels: none -> 278 us  [the longest x1 246 us: exchange(): pl.pallas_call(functools.partial(exchange_kernel, dims, plan(dims, orders...]
    all_to_all x4 -> x1, waiting for transfers between devices: 270 us -> 6.57 us  [body(): lax.all_to_all(derivs.reshape(n_experts, n_tokens), 'expert', split_axis=...]
    all_to_all x4 -> x1, starting transfers between devices: 86 us -> 25.6 us  [body(): lax.all_to_all(derivs.reshape(n_experts, n_tokens), 'expert', split_axis=...]
    gather x4 -> x0, local copies, waits for them, and re-layouts: 30.9 us -> none  [the longest x1 9.54 us: body(): grad_rows[safe_index // n_routes]]
    dot_general x3 -> x2, matrix products: 40.3 us -> 25.3 us  [the longest x1 23.2 us: body(): lax.dot_general(hidden, grads, (((0,), (0,)), ((), ())), preferred_elemen...]
    select_n x5 -> x0, other arithmetic: 13.9 us -> none  [the longest x1 10.6 us: body(): jnp.where(filled[:, None], grad_rows[safe_index // n_routes], jnp.zeros((...]
    convert_element_type x1 -> x0, local copies, waits for them, and re-layouts: 6.65 us -> none  [expert_derivs(): return jnp.sum(projected * hidden_in.astype(jnp.float32), axis=1)]
    convert_element_type x4 -> x2, other arithmetic: 5.36 us -> 0.61 us  [the longest x1 0.6 us: spread(): weights_low.astype(jnp.float32).reshape(steps, 1, cols)]
  transfers between devices with their start and end apart: 5 -> 4, of which waited for: 3 -> 1; matrix products, arithmetic and copies ran while one was open for 15% -> 7% of each run, Pallas kernels for 0% -> 0%
where the time goes in v1:
time: 342 us
  Pallas kernels  278 us (81%)
  starting transfers between devices  26.2 us (8%)
  matrix products  25.3 us (7%)
  waiting for transfers between devices  6.57 us (2%)
    pallas_call x1, Pallas kernels, exchange(): pl.pallas_call(functools.partial(exchange_kernel, dims, plan(dims, orders...  246 us
    all_to_all x1, starting transfers between devices, body(): lax.all_to_all(derivs.reshape(n_experts, n_tokens), 'expert', split_axis=...  25.6 us
    pallas_call x1, Pallas kernels, derivs_of(): pl.pallas_call(deriv_kernel, grid=(rows // tile,), out_shape=jax.ShapeDty...  23.5 us
    dot_general x1, matrix products, body(): lax.dot_general(hidden, grads, (((0,), (0,)), ((), ())), preferred_elemen...  23.2 us
    pallas_call x1, Pallas kernels, spread(): pl.pallas_call(functools.partial(spread_kernel, n_experts, group, top), g...  8.66 us
  transfers between devices with their start and end apart: 4, of which 1 were waited for; matrix products, arithmetic and copies ran while one was open for 7% of the time, Pallas kernels for 0%

profile of v1, /device:TPU:0, one launch (start us, length us, event | category | flops | bytes accessed | tf_op | source)
XLA Modules:
  0.0 341.6 jit_solution(1496765866692276396)
XLA Ops:
  0.6 0.8 copy.27
  1.4 0.7 reduce_sum.36
  2.1 0.1 div.34
  2.2 0.1 div.35
  2.3 0.1 div.36
  2.4 0.1 squeeze.17
  2.5 0.6 copy_convert_fusion.weight_ref
  3.1 0.8 copy.29
  3.9 0.7 reshape_squeeze.11
  4.6 8.7 %spread.1.dense_ref = bf16[16,128,1024]{2,1,0:T(8,128)(2,1)} custom-call(bf16[1024,1024]{1,0:T(8,128)(2,1)} %bitcast.36, f32[8,1,128]{2,1,0:T(1,128)} %copy_convert_fusion.weight_ref, s32[8,1,128]{2,1,0:T(1,128)} %bitcast.41), custom_call_target="tpu_custom_call" | custom-call | tf_op jit(solution)/shard_map/spread/pallas_call | solution.py:231
  13.2 245.6 %exchange.1 = (bf16[16,4,32,4096]{3,2,1,0:T(8,128)(2,1)}, bf16[16,128,1024]{2,1,0:T(8,128)(2,1)}) custom-call(bf16[4,32,4096]{2,1,0:T(8,128)(2,1)} %bitcast.37, bf16[16,128,1024]{2,1,0:T(8,128)(2,1)} %spread.1.dense_ref), custom_call_target="tpu_custom_call" | custom-call | tf_op jit(solution)/shard_map/exchange/pallas_call | solution.py:190
  258.9 0.0 copy-start
  258.9 0.0 copy-start.3
  258.9 0.0 copy-start.1
  258.9 0.0 copy-start.2
  258.9 23.5 %derivs.1 = f32[2048,1]{1,0:T(8,128)S(1)} custom-call(bf16[2048,4096]{1,0:T(8,128)(2,1)} %bitcast.43, bf16[2048,1024]{1,0:T(8,128)(2,1)} %bitcast.46, bf16[1024,4096]{1,0:T(8,128)(2,1)} %bitcast.45), custom_call_target="tpu_custom_call" | custom-call | flops 17179869184 | bytes 16777216 | tf_op jit(solution)/shard_map/derivs/pallas_call | solution.py:260
  282.4 0.9 reduce.1
  283.3 25.6 %all-to-all-start = ((f32[16,1,128]{2,1,0:T(1,128)}), f32[16,1,128]{2,1,0:T(1,128)S(1)}, u32[]{:S(2)}, u32[]{:S(2)}) async-start(f32[16,1,128]{2,1,0:T(1,128)} %bitcast.12), calls=%async_computation | async-start | bytes 16384 | tf_op jit(solution)/shard_map/all_to_all | solution.py:299
  308.9 0.0 copy-done
  308.9 0.1 collective-permute-start
  309.0 0.0 copy-done.3
  309.0 0.5 collective-permute-start.2
  309.5 0.0 copy-done.1
  309.5 0.0 copy-done.2
  309.6 6.6 %all-to-all-done = f32[16,1,128]{2,1,0:T(1,128)S(1)} async-done(((f32[16,1,128]{2,1,0:T(1,128)}), f32[16,1,128]{2,1,0:T(1,128)S(1)}, u32[]{:S(2)}, u32[]{:S(2)}) %all-to-all-start) | async-done | bytes 8224 | tf_op jit(solution)/shard_map/all_to_all | solution.py:299
  316.2 0.1 collective-permute-start.1
  316.2 23.2 %convert_bitcast_fusion = bf16[1,1,1024,4096]{3,2,1,0:T(8,128)(2,1)} fusion(bf16[2048,1024]{1,0:T(8,128)(2,1)} %bitcast.47, bf16[2048,4096]{1,0:T(8,128)(2,1)} %bitcast.44), kind=kOutput, calls=%fused_computation | convolution fusion | flops 17184063488 | bytes 29360128 | tf_op jit(solution)/shard_map/dot_general | solution.py:302
  339.5 0.0 collective-permute-done.1
  339.5 0.0 collective-permute-done.2
  339.5 0.0 collective-permute-done
  339.5 2.1 fusion
  (5 shorter events, 0.1 us)
Async XLA Ops:
  258.9 50.0 %copy-start = (bf16[1,128,4096]{2,1,0:T(8,128)(2,1)S(1)}, bf16[1,128,4096]{2,1,0:T(8,128)(2,1)}, u32[]{:S(2)}) copy-start(bf16[1,128,4096]{2,1,0:T(8,128)(2,1)} %param.6) | copy-start | bytes 3145732
  258.9 50.1 %copy-start.3 = (bf16[1,16,4096]{2,1,0:T(8,128)(2,1)S(1)}, bf16[1,16,4096]{2,1,0:T(8,128)(2,1)}, u32[]{:S(2)}) copy-start(bf16[1,16,4096]{2,1,0:T(8,128)(2,1)} %param.11) | copy-start | bytes 393220
  258.9 50.6 %copy-start.1 = (f32[1,128,8]{1,2,0:T(8,128)S(1)}, f32[1,128,8]{1,2,0:T(8,128)}, u32[]{:S(2)}) copy-start(f32[1,128,8]{1,2,0:T(8,128)} %param.9) | copy-start | bytes 12292
  258.9 50.6 %copy-start.2 = (s32[1,128,8]{1,2,0:T(8,128)S(1)}, s32[1,128,8]{1,2,0:T(8,128)}, u32[]{:S(2)}) copy-start(s32[1,128,8]{1,2,0:T(8,128)} %param.8) | copy-start | bytes 12292
  283.3 32.8 %all-to-all-start = ((f32[16,1,128]{2,1,0:T(1,128)}), f32[16,1,128]{2,1,0:T(1,128)S(1)}, u32[]{:S(2)}, u32[]{:S(2)}) async-start(f32[16,1,128]{2,1,0:T(1,128)} %bitcast.12), calls=%async_computation | async-start | bytes 16384 | tf_op jit(solution)/shard_map/all_to_all | solution.py:299
  308.9 30.6 %collective-permute-start = (bf16[128,4096]{1,0:T(8,128)(2,1)S(1)}, bf16[128,4096]{1,0:T(8,128)(2,1)S(1)}, u32[]{:S(2)}, u32[]{:S(2)}) collective-permute-start(bf16[128,4096]{1,0:T(8,128)(2,1)S(1)} %bitcast.38), channel_id=1, source_target_pairs={{0,16},{16,0},{1,17},{17,1},{2,18},{18,2},{3,19},{19,3},{4,20},{20... | collective-permute-start | bytes 3145736 | tf_op jit(solution)/shard_map/ppermute | solution.py:280
  309.0 30.5 %collective-permute-start.2 = (bf16[16,4096]{1,0:T(8,128)(2,1)S(1)}, bf16[16,4096]{1,0:T(8,128)(2,1)S(1)}, u32[]{:S(2)}, u32[]{:S(2)}) collective-permute-start(bf16[16,4096]{1,0:T(8,128)(2,1)S(1)} %bitcast.48), channel_id=1, source_target_pairs={{0,16},{16,0},{1,17},{17,1},{2,18},{18,2},{3,19},{19,3},{4,20},{20... | collective-permute-start | bytes 393224 | tf_op jit(solution)/shard_map/ppermute | solution.py:280
  316.2 23.3 %collective-permute-start.1 = (f32[16,128]{1,0:T(8,128)S(1)}, f32[16,128]{1,0:T(8,128)S(1)}, u32[]{:S(2)}, u32[]{:S(2)}) collective-permute-start(f32[16,128]{1,0:T(8,128)S(1)} %subtract_multiply_fusion), channel_id=1, source_target_pairs={{0,16},{16,0},{1,17},{17,1},{2,18},{18,2},{3,19},{19,3},{4,20},{20... | collective-permute-start | bytes 24584 | tf_op jit(solution)/shard_map/ppermute | solution.py:280

commit v2 on v1

--- a/solution.py
+++ b/solution.py
@@ -179,16 +179,147 @@
         store.wait()
 
 
+def line_kernel(dims, orders, grad_ref, dense_ref, all_ref, got_ref, own, own_dense, g_send, g_recv, h_send, h_recv, local):
+    n = dims[0] * dims[1] * dims[2]
+    chunks = len(orders)
+    me = lax.axis_index("expert")
+    here = [me // (dims[1] * dims[2]), (me // dims[2]) % dims[1], me % dims[2]]
+
+    def number(c):
+        return (c[0] * dims[1] + c[1]) * dims[2] + c[2]
+
+    load = pltpu.make_async_copy(grad_ref, own, local.at[0])
+    load.start()
+    load_dense = pltpu.make_async_copy(dense_ref.at[me], own_dense, local.at[1])
+    load_dense.start()
+    barrier = pltpu.get_barrier_semaphore()
+    for i in range(1, n):
+        pl.semaphore_signal(barrier, inc=1, device_id={"expert": (me + i) % n}, device_id_type=MESH)
+    pl.semaphore_wait(barrier, n - 1)
+    load.wait()
+
+    def start(source, chunk, axis, step, home):
+        target = list(here)
+        target[axis] = (here[axis] + step) % dims[axis]
+        pltpu.make_async_remote_copy(
+            src_ref=own.at[chunk] if home else all_ref.at[source, chunk],
+            dst_ref=all_ref.at[source, chunk],
+            send_sem=g_send.at[source, chunk, axis, (step + 1) // 2],
+            recv_sem=g_recv.at[source, chunk],
+            device_id={"expert": number(target)},
+            device_id_type=MESH,
+        ).start()
+
+    def finish(source, chunk, axis, step, home):
+        piece = own.at[chunk] if home else all_ref.at[source, chunk]
+        pltpu.make_async_copy(piece, piece, g_send.at[source, chunk, axis, (step + 1) // 2]).wait()
+
+    def moves(offset, order):
+        last = max([i for i in range(3) if offset[order[i]] != 0], default=-1)
+        steps = []
+        if last >= 0 and dims[order[last]] > 2:
+            steps.append((order[last], 1 if offset[order[last]] > 0 else -1))
+        for axis in order[last + 1 :]:
+            if dims[axis] == 2:
+                steps.append((axis, 1))
+            elif dims[axis] > 2:
+                steps += [(axis, 1), (axis, -1)]
+        return steps
+
+    def each_move(offset, order, chunk, act):
+        source = number([(here[i] - offset[i] + dims[i]) % dims[i] for i in range(3)])
+        home = offset == (0, 0, 0)
+        for axis, step in moves(offset, order):
+            if dims[axis] == 2:
+                act(source, chunk, axis, step, home)
+            else:
+                inside = here[axis] < dims[axis] - 1 if step > 0 else here[axis] > 0
+                pl.when(inside)(functools.partial(act, source, chunk, axis, step, home))
+
+    def on_slice(offset, act):
+        valid = None
+        for i in range(3):
+            if dims[i] > 2 and offset[i] != 0:
+                inside = here[i] >= offset[i] if offset[i] > 0 else here[i] < dims[i] + offset[i]
+                valid = inside if valid is None else valid & inside
+        if valid is None:
+            act()
+        else:
+            pl.when(valid)(act)
+
+    spans = [range(size) if size <= 2 else range(1 - size, size) for size in dims]
+    offsets = [(a, b, c) for a in spans[0] for b in spans[1] for c in spans[2] if (a, b, c) != (0, 0, 0)]
+
+    for chunk in range(chunks):
+        each_move((0, 0, 0), orders[chunk], chunk, start)
+
+    def dense_copy(k):
+        return pltpu.make_async_remote_copy(
+            src_ref=dense_ref.at[(me + k) % n],
+            dst_ref=got_ref.at[me],
+            send_sem=h_send.at[k],
+            recv_sem=h_recv.at[k],
+            device_id={"expert": (me + k) % n},
+            device_id_type=MESH,
+        )
+
+    store = pltpu.make_async_copy(own, all_ref.at[me], local.at[2])
+    store.start()
+    load_dense.wait()
+    store_dense = pltpu.make_async_copy(own_dense, got_ref.at[me], local.at[3])
+    store_dense.start()
+
+    arrivals = []
+    for chunk in range(chunks):
+        for offset in offsets:
+            hops = [abs(offset[axis]) for axis in orders[chunk]]
+            arrivals.append((hops[0] * WEIGHTS[0] + hops[1] * WEIGHTS[1] + hops[2] * WEIGHTS[2], chunk, offset))
+    arrivals.sort()
+    far = sorted(range(1, n), key=lambda k: -min(k, n - k))
+    every = max(1, (len(arrivals) * SHARE // 4) // len(far))
+    for count, (_, chunk, offset) in enumerate(arrivals):
+        if count % every == 0 and far:
+            dense_copy(far.pop(0)).start()
+
+        def arrive(chunk=chunk, offset=offset):
+            source = number([(here[i] - offset[i] + dims[i]) % dims[i] for i in range(3)])
+            piece = all_ref.at[source, chunk]
+            pltpu.make_async_copy(piece, piece, g_recv.at[source, chunk]).wait()
+            each_move(offset, orders[chunk], chunk, start)
+
+        on_slice(offset, arrive)
+    for k in far:
+        dense_copy(k).start()
+    for k in range(1, n):
+        dense_copy(k).wait()
+    for chunk in range(chunks):
+        each_move((0, 0, 0), orders[chunk], chunk, finish)
+        for offset in offsets:
+            if moves(offset, orders[chunk]):
+                on_slice(offset, functools.partial(each_move, offset, orders[chunk], chunk, finish))
+    store.wait()
+    store_dense.wait()
+
+
+WEIGHTS = (2, 3, 3)
+SHARE = 3
+LINE_ORDERS = ((0, 2, 1), (0, 1, 2), (0, 2, 1), (0, 1, 2))
+
+
 def exchange(grad_rows, dense):
     n, n_tokens, hidden_width = dense.shape
     width = grad_rows.shape[1]
     dims = torus_dims(n)
+    on_line = 2 in dims
     orders = [((2, 1, 0), 0), ((1, 2, 0), 1), ((0, 2, 1), 0), ((0, 1, 2), 1)]
-    chunks = len(orders)
+    if on_line:
+        kernel, chunks = functools.partial(line_kernel, dims, LINE_ORDERS), len(LINE_ORDERS)
+    else:
+        kernel, chunks = functools.partial(exchange_kernel, dims, plan(dims, orders)), len(orders)
     rows = n_tokens // chunks
     grad_chunks = grad_rows.reshape(chunks, rows, width)
     got, dense_got = pl.pallas_call(
-        functools.partial(exchange_kernel, dims, plan(dims, orders)),
+        kernel,
         out_shape=(
             jax.ShapeDtypeStruct((n, chunks, rows, width), grad_rows.dtype),
             jax.ShapeDtypeStruct(dense.shape, dense.dtype),
@@ -198,7 +329,7 @@
         scratch_shapes=[
             pltpu.VMEM((chunks, rows, width), grad_rows.dtype),
             pltpu.VMEM((n_tokens, hidden_width), dense.dtype),
-            pltpu.SemaphoreType.DMA((n, chunks)),
+            pltpu.SemaphoreType.DMA((n, chunks, 3, 2) if on_line else (n, chunks)),
             pltpu.SemaphoreType.DMA((n, chunks)),
             pltpu.SemaphoreType.DMA((n,)),
             pltpu.SemaphoreType.DMA((n,)),

time: 342 us -> 272 us (0.80)
  Pallas kernels: 278 us -> 224 us
  starting transfers between devices: 26.2 us -> 9.13 us
    pallas_call x1, Pallas kernels: 246 us -> 192 us  [exchange(): pl.pallas_call(kernel, out_shape=(jax.ShapeDtypeStruct((n, chunks, rows,...]
    all_to_all x1, starting transfers between devices: 25.6 us -> 8.5 us  [body(): lax.all_to_all(derivs.reshape(n_experts, n_tokens), 'expert', split_axis=...]
  transfers between devices with their start and end apart: 4 -> 4, of which waited for: 1 -> 1; matrix products, arithmetic and copies ran while one was open for 7% -> 9% of each run, Pallas kernels for 0% -> 0%
where the time goes in v2:
time: 272 us; the launch traced here: 271 us
  Pallas kernels  224 us (82%)
  matrix products  25.3 us (9%)
  starting transfers between devices  9.13 us (3%)
  waiting for transfers between devices  6.57 us (2%)
    pallas_call x1, Pallas kernels, exchange(): pl.pallas_call(kernel, out_shape=(jax.ShapeDtypeStruct((n, chunks, rows,...  192 us
    pallas_call x1, Pallas kernels, derivs_of(): pl.pallas_call(deriv_kernel, grid=(rows // tile,), out_shape=jax.ShapeDty...  23.5 us
    dot_general x1, matrix products, body(): lax.dot_general(hidden, grads, (((0,), (0,)), ((), ())), preferred_elemen...  23.2 us
    pallas_call x1, Pallas kernels, spread(): pl.pallas_call(functools.partial(spread_kernel, n_experts, group, top), g...  8.66 us
    all_to_all x1, starting transfers between devices, body(): lax.all_to_all(derivs.reshape(n_experts, n_tokens), 'expert', split_axis=...  8.5 us
    all_to_all x1, waiting for transfers between devices, body(): lax.all_to_all(derivs.reshape(n_experts, n_tokens), 'expert', split_axis=...  6.56 us
  transfers between devices with their start and end apart: 4, of which 1 were waited for; matrix products, arithmetic and copies ran while one was open for 9% of the time, Pallas kernels for 0%

profile of v2, /device:TPU:0, one launch (start us, length us, event | category | flops | bytes accessed | tf_op | source)
XLA Modules:
  0.0 271.2 jit_solution(4954972038421737240)
XLA Ops:
  0.6 0.8 copy.27
  1.4 0.7 reduce_sum.36
  2.1 0.1 div.34
  2.2 0.1 div.35
  2.3 0.1 div.36
  2.4 0.1 squeeze.17
  2.5 0.6 copy_convert_fusion.weight_ref
  3.1 0.8 copy.29
  3.9 0.7 reshape_squeeze.11
  4.6 8.7 %spread.1.dense_ref = bf16[16,128,1024]{2,1,0:T(8,128)(2,1)} custom-call(bf16[1024,1024]{1,0:T(8,128)(2,1)} %bitcast.36, f32[8,1,128]{2,1,0:T(1,128)} %copy_convert_fusion.weight_ref, s32[8,1,128]{2,1,0:T(1,128)} %bitcast.41), custom_call_target="tpu_custom_call" | custom-call | tf_op jit(solution)/shard_map/spread/pallas_call | solution.py:362
  13.2 192.3 %exchange.1 = (bf16[16,4,32,4096]{3,2,1,0:T(8,128)(2,1)}, bf16[16,128,1024]{2,1,0:T(8,128)(2,1)}) custom-call(bf16[4,32,4096]{2,1,0:T(8,128)(2,1)} %bitcast.37, bf16[16,128,1024]{2,1,0:T(8,128)(2,1)} %spread.1.dense_ref), custom_call_target="tpu_custom_call" | custom-call | tf_op jit(solution)/shard_map/exchange/pallas_call | solution.py:321
  205.6 0.0 copy-start
  205.6 0.0 copy-start.3
  205.6 0.0 copy-start.1
  205.6 0.0 copy-start.2
  205.6 23.5 %derivs.1 = f32[2048,1]{1,0:T(8,128)S(1)} custom-call(bf16[2048,4096]{1,0:T(8,128)(2,1)} %bitcast.43, bf16[2048,1024]{1,0:T(8,128)(2,1)} %bitcast.46, bf16[1024,4096]{1,0:T(8,128)(2,1)} %bitcast.45), custom_call_target="tpu_custom_call" | custom-call | flops 17179869184 | bytes 16777216 | tf_op jit(solution)/shard_map/derivs/pallas_call | solution.py:391
  229.1 0.9 reduce.1
  230.0 8.5 %all-to-all-start = ((f32[16,1,128]{2,1,0:T(1,128)}), f32[16,1,128]{2,1,0:T(1,128)S(1)}, u32[]{:S(2)}, u32[]{:S(2)}) async-start(f32[16,1,128]{2,1,0:T(1,128)} %bitcast.12), calls=%async_computation | async-start | bytes 16384 | tf_op jit(solution)/shard_map/all_to_all | solution.py:430
  238.6 0.0 copy-done
  238.6 0.1 collective-permute-start
  238.6 0.0 copy-done.3
  238.7 0.5 collective-permute-start.2
  239.1 0.0 copy-done.1
  239.2 0.0 copy-done.2
  239.2 6.6 %all-to-all-done = f32[16,1,128]{2,1,0:T(1,128)S(1)} async-done(((f32[16,1,128]{2,1,0:T(1,128)}), f32[16,1,128]{2,1,0:T(1,128)S(1)}, u32[]{:S(2)}, u32[]{:S(2)}) %all-to-all-start) | async-done | bytes 8224 | tf_op jit(solution)/shard_map/all_to_all | solution.py:430
  245.8 0.1 collective-permute-start.1
  245.9 23.2 %convert_bitcast_fusion = bf16[1,1,1024,4096]{3,2,1,0:T(8,128)(2,1)} fusion(bf16[2048,1024]{1,0:T(8,128)(2,1)} %bitcast.47, bf16[2048,4096]{1,0:T(8,128)(2,1)} %bitcast.44), kind=kOutput, calls=%fused_computation | convolution fusion | flops 17184063488 | bytes 29360128 | tf_op jit(solution)/shard_map/dot_general | solution.py:433
  269.1 0.0 collective-permute-done.1
  269.1 0.0 collective-permute-done.2
  269.1 0.0 collective-permute-done
  269.1 2.1 fusion
  (5 shorter events, 0.1 us)
Async XLA Ops:
  205.6 33.0 %copy-start = (bf16[1,128,4096]{2,1,0:T(8,128)(2,1)S(1)}, bf16[1,128,4096]{2,1,0:T(8,128)(2,1)}, u32[]{:S(2)}) copy-start(bf16[1,128,4096]{2,1,0:T(8,128)(2,1)} %param.6) | copy-start | bytes 3145732
  205.6 33.1 %copy-start.3 = (bf16[1,16,4096]{2,1,0:T(8,128)(2,1)S(1)}, bf16[1,16,4096]{2,1,0:T(8,128)(2,1)}, u32[]{:S(2)}) copy-start(bf16[1,16,4096]{2,1,0:T(8,128)(2,1)} %param.11) | copy-start | bytes 393220
  205.6 33.6 %copy-start.1 = (f32[1,128,8]{1,2,0:T(8,128)S(1)}, f32[1,128,8]{1,2,0:T(8,128)}, u32[]{:S(2)}) copy-start(f32[1,128,8]{1,2,0:T(8,128)} %param.9) | copy-start | bytes 12292
  205.6 33.6 %copy-start.2 = (s32[1,128,8]{1,2,0:T(8,128)S(1)}, s32[1,128,8]{1,2,0:T(8,128)}, u32[]{:S(2)}) copy-start(s32[1,128,8]{1,2,0:T(8,128)} %param.8) | copy-start | bytes 12292
  230.0 15.7 %all-to-all-start = ((f32[16,1,128]{2,1,0:T(1,128)}), f32[16,1,128]{2,1,0:T(1,128)S(1)}, u32[]{:S(2)}, u32[]{:S(2)}) async-start(f32[16,1,128]{2,1,0:T(1,128)} %bitcast.12), calls=%async_computation | async-start | bytes 16384 | tf_op jit(solution)/shard_map/all_to_all | solution.py:430
  238.6 30.6 %collective-permute-start = (bf16[128,4096]{1,0:T(8,128)(2,1)S(1)}, bf16[128,4096]{1,0:T(8,128)(2,1)S(1)}, u32[]{:S(2)}, u32[]{:S(2)}) collective-permute-start(bf16[128,4096]{1,0:T(8,128)(2,1)S(1)} %bitcast.38), channel_id=1, source_target_pairs={{0,16},{16,0},{1,17},{17,1},{2,18},{18,2},{3,19},{19,3},{4,20},{20... | collective-permute-start | bytes 3145736 | tf_op jit(solution)/shard_map/ppermute | solution.py:411
  238.7 30.5 %collective-permute-start.2 = (bf16[16,4096]{1,0:T(8,128)(2,1)S(1)}, bf16[16,4096]{1,0:T(8,128)(2,1)S(1)}, u32[]{:S(2)}, u32[]{:S(2)}) collective-permute-start(bf16[16,4096]{1,0:T(8,128)(2,1)S(1)} %bitcast.48), channel_id=1, source_target_pairs={{0,16},{16,0},{1,17},{17,1},{2,18},{18,2},{3,19},{19,3},{4,20},{20... | collective-permute-start | bytes 393224 | tf_op jit(solution)/shard_map/ppermute | solution.py:411
  245.8 23.3 %collective-permute-start.1 = (f32[16,128]{1,0:T(8,128)S(1)}, f32[16,128]{1,0:T(8,128)S(1)}, u32[]{:S(2)}, u32[]{:S(2)}) collective-permute-start(f32[16,128]{1,0:T(8,128)S(1)} %subtract_multiply_fusion), channel_id=1, source_target_pairs={{0,16},{16,0},{1,17},{17,1},{2,18},{18,2},{3,19},{19,3},{4,20},{20... | collective-permute-start | bytes 24584 | tf_op jit(solution)/shard_map/ppermute | solution.py:411
